TPU v7x, 512 devices: a whole 4x8x8 slice. The times are simulated.
512 devices in a mesh: dp: 32 (over x_lo, y, core), slab: 16 (over x_hi, z).
Axes of the slice: x: 4 (x_hi: 2, x_lo: 2; x = x_hi * 2 + x_lo), y: 8, z: 8, core: 2. Of those that a mesh axis runs over, the one named last changes fastest.
Arguments:
- activation: bfloat16 [128, 64, 128, 256], P('dp', None, 'slab'), may hold values from -6 to 6
- cotangent: bfloat16 [128, 64, 128, 256], P('dp', None, 'slab'), may hold values from -6 to 6
- spectral_weight: bfloat16 [64, 32, 32, 128], P(None, 'slab'), may hold values from -0.75 to 0.75
Outputs:
- input_grad: bfloat16 [128, 64, 128, 256], P('dp', None, 'slab')
- weight_grad: float32 [64, 32, 32, 128], P('dp', 'slab')
All inputs are finite; a program needn't handle non-finite values.
Results may differ from a plain program's by a relative error of at most 0.023.
Values may be sent and summed in bfloat16 or wider, within the bound.
A program may use at most 64 MiB of HBM per device.

v0:
```python
import math

import jax
import jax.numpy as jnp
from jax import lax
from jax.sharding import PartitionSpec as P


def in_blocks(array, dim, size):
    before, after = (array.shape[:dim], array.shape[dim + 1 :])
    return jnp.moveaxis(array.reshape(*before, size, -1, *after), dim, 0)


def summed_on_arrival(array, axis, dim):
    size = lax.axis_size(axis)
    tiles = lax.all_to_all(in_blocks(array, dim, size), axis, 0, 0, tiled=True)
    return jnp.sum(tiles.astype(jnp.float32), axis=0)


def retained(length, modes):
    index = jnp.arange(modes, dtype=jnp.int32)
    return jnp.where(index < modes // 2, index, index + (length - modes))


def cos_sin(length, modes):
    cells = jnp.arange(length, dtype=jnp.int32)
    phase = cells[:, None] * retained(length, modes)[None, :] % length
    angle = phase.astype(jnp.float32) * (2.0 * math.pi / length)
    factor = 1.0 / math.sqrt(length)
    return (
        (jnp.cos(angle) * factor).astype(jnp.bfloat16),
        (jnp.sin(angle) * factor).astype(jnp.bfloat16),
    )


def y_table(cosine_table, sine_table):
    upper = jnp.concatenate([cosine_table, -sine_table], axis=1)
    lower = jnp.concatenate([sine_table, cosine_table], axis=1)
    return jnp.concatenate([upper, lower], axis=0)


def x_table(cosine_table, sine_table):
    first = jnp.stack([cosine_table, -sine_table], axis=2)
    second = jnp.stack([sine_table, cosine_table], axis=2)
    return jnp.stack([first, second], axis=1)


def paired_out(spectra_out, channels):
    modes_here, amount, modes_x = spectra_out.shape[:3]
    split = spectra_out.reshape(modes_here, amount, modes_x, 2, channels)
    swapped = jnp.stack([split[:, :, :, 1], -split[:, :, :, 0]], axis=3)
    return jnp.concatenate([split, swapped], axis=4)


def body(activation, cotangent, spectral_weight):
    slabs = lax.axis_size("slab")
    samples, channels, rows_here, double_y = activation.shape
    y_length = double_y // 2
    x_length = rows_here * slabs
    modes_here = spectral_weight.shape[1]
    modes_y = modes_here * slabs
    modes_x = spectral_weight.shape[2]
    cos_y, sin_y = cos_sin(y_length, modes_y)
    cos_x, sin_x = cos_sin(x_length, modes_x)
    table_y = y_table(cos_y, sin_y).reshape(2 * y_length, 2, slabs, modes_here)
    table_y = table_y.transpose(0, 2, 1, 3).reshape(2 * y_length, 2 * modes_y)
    table_x = x_table(cos_x, sin_x)
    table_slabs = table_x.reshape(slabs, rows_here, 2, modes_x, 2)

    def to_modes(volume):
        along = jnp.einsum("ys,bcry->sbcr", table_y, volume, preferred_element_type=jnp.float32)
        along = along.astype(jnp.bfloat16)
        return along.reshape(slabs, 2 * modes_here, samples, channels * rows_here)

    members = (
        lax.all_to_all(to_modes(activation), "slab", split_axis=0, concat_axis=0, tiled=True),
        lax.all_to_all(to_modes(cotangent), "slab", split_axis=0, concat_axis=0, tiled=True),
    )
    results = []
    for member in members:
        amount = member.shape[2]
        layout = member.reshape(slabs, 2, modes_here, amount, channels, rows_here)
        spectra = jnp.einsum(
            "sptbcr,srpkq->tbkqc", layout, table_slabs, preferred_element_type=jnp.float32
        )
        results.append(
            spectra.astype(jnp.bfloat16).reshape(modes_here, amount, modes_x, 2 * channels)
        )
    spec_in, spec_out = tuple(results)
    inputs_split = spec_in.reshape(modes_here, samples, modes_x, 2, channels)
    paired = paired_out(spec_out, channels)
    weight_grad = summed_on_arrival(
        jnp.einsum(
            "tbkqi,tbkqn->itkn", inputs_split, paired, preferred_element_type=jnp.float32
        ).astype(jnp.bfloat16),
        "dp",
        0,
    )
    inputs_paired = paired_out(spec_out, channels)
    stacked = jnp.stack([inputs_paired[..., :channels], inputs_paired[..., channels:]], axis=3)
    stacked = stacked.transpose(0, 1, 2, 4, 3, 5).reshape(
        modes_here, samples, modes_x, 2, 2 * channels
    )
    spec_grad = jnp.einsum(
        "tbkrn,itkn->tbkri", stacked, spectral_weight, preferred_element_type=jnp.float32
    )
    spec_grad = spec_grad.astype(jnp.bfloat16)
    spread = jnp.einsum(
        "tbkqi,srpkq->sptbir", spec_grad, table_slabs, preferred_element_type=jnp.float32
    )
    spread = spread.astype(jnp.bfloat16).reshape(
        slabs, 2 * modes_here, samples, channels * rows_here
    )
    member = lax.all_to_all(spread, "slab", split_axis=0, concat_axis=0, tiled=True)
    amount = member.shape[2]
    lines = member.reshape(2 * modes_y, amount, channels, rows_here)
    values = jnp.einsum("sbcr,ys->bcry", lines, table_y, preferred_element_type=jnp.float32)
    input_grad = values.astype(jnp.bfloat16)
    return (input_grad, weight_grad)


def solution(mesh):
    placed = (P("dp", None, "slab", None), P("dp", None, "slab", None), P(None, "slab", None, None))
    return jax.shard_map(
        body,
        mesh=mesh,
        in_specs=placed,
        out_specs=(P("dp", None, "slab", None), P("dp", "slab", None, None)),
        check_vma=False,
    )
```

profile of v0, /device:TPU:1, one launch (start us, length us, event | category | flops | bytes accessed | tf_op | source)
XLA Modules:
  0.0 120.6 jit_solution(5014927930415409145)
XLA Ops:
  0.6 0.0 copy-start
  0.7 0.2 multiply_convert_fusion.2
  0.8 0.2 fusion.35
  1.1 1.9 %convolution_convert_fusion.1 = bf16[64,4,64,8]{2,0,3,1:T(8,128)(2,1)S(1)} fusion(bf16[4,64,8,256]{3,2,1,0:T(8,128)(2,1)} %param.4, bf16[256,64,1,1]{0,1,2,3:T(8,128)(2,1)S(1)} %reshape.172), kind=kOutput, calls=%fused_computation.8 | convolution fusion | flops 67239936 | bytes 1343488 | tf_op jit(solution)/shard_map/ys,bcry->sbcr/dot_general | solution.py:71
  2.9 0.0 copy-start.1
  2.9 3.2 %copy.47 = bf16[64,4,64,8]{3,2,1,0:T(8,128)(2,1)} copy(bf16[64,4,64,8]{2,0,3,1:T(8,128)(2,1)S(1)} %convolution_convert_fusion.1) | data formatting | bytes 524288 | tf_op jit(solution)/shard_map/convert_element_type | solution.py:72
  6.2 6.9 %reshape.164 = bf16[16,4,4,512]{3,2,1,0:T(4,128)(2,1)} reshape(bf16[64,4,64,8]{3,2,1,0:T(8,128)(2,1)} %copy.47) | data formatting | bytes 524288 | tf_op jit(solution)/shard_map/reshape | solution.py:73
  13.0 13.4 %all-to-all-start = ((bf16[16,4,4,512]{3,2,1,0:T(4,128)(2,1)}), bf16[16,4,4,512]{3,2,1,0:T(4,128)(2,1)S(1)}, u32[]{:S(2)}, u32[]{:S(2)}) async-start(bf16[16,4,4,512]{3,2,1,0:T(4,128)(2,1)} %reshape.164), calls=%async_computation | async-start | bytes 524288 | tf_op jit(solution)/shard_map/all_to_all | solution.py:77
  26.5 0.0 copy-done.1
  26.5 0.6 convolution_convert_fusion
  27.1 3.2 %copy.59 = bf16[64,4,64,8]{3,2,1,0:T(8,128)(2,1)} copy(bf16[64,4,64,8]{2,0,3,1:T(8,128)(2,1)S(1)} %convolution_convert_fusion) | data formatting | bytes 524288 | tf_op jit(solution)/shard_map/convert_element_type | solution.py:72
  30.3 6.9 %reshape.169 = bf16[16,4,4,512]{3,2,1,0:T(4,128)(2,1)} reshape(bf16[64,4,64,8]{3,2,1,0:T(8,128)(2,1)} %copy.59) | data formatting | bytes 524288 | tf_op jit(solution)/shard_map/reshape | solution.py:73
  37.2 0.3 fusion.34
  37.6 0.3 multiply_convert_fusion
  37.9 0.0 all-to-all-done
  37.9 9.1 %all-to-all-start.2 = ((bf16[16,4,4,512]{3,2,1,0:T(4,128)(2,1)}), bf16[16,4,4,512]{3,2,1,0:T(4,128)(2,1)}, u32[]{:S(2)}, u32[]{:S(2)}) async-start(bf16[16,4,4,512]{3,2,1,0:T(4,128)(2,1)} %reshape.169), calls=%async_computation.2 | async-start | bytes 524288 | tf_op jit(solution)/shard_map/all_to_all | solution.py:76
  47.1 1.1 copy.48
  48.1 1.8 %copy.49 = bf16[16,2,2,4,64,8]{4,0,5,1,3,2:T(8,128)(2,1)} copy(bf16[16,2,2,4,64,8]{0,5,4,3,2,1:T(8,128)(2,1)S(1)} %bitcast.83) | data formatting | bytes 524288 | tf_op jit(solution)/shard_map/reshape | solution.py:82
  49.9 1.3 %fusion.7 = bf16[32,2,2,4,64]{4,0,3,2,1:T(8,128)(2,1)S(1)} fusion(bf16[16,2,2,4,64,8]{4,0,5,1,3,2:T(8,128)(2,1)} %copy.49, bf16[16,8,1,32,1]{3,0,1,2,4:T(8,128)(2,1)S(1)} %get-tuple-element.9, bf16[16,8,1,32,1]{3,0,1,2,4:T(8,128)(2,1)S(1)} %get-tuple-element.8, bf16[16,8,1,32,1]{3,0,1,2,4:T(8,128)(2,1)S(1)} %fusion.34), kind=kOutput, calls=%fused_computation.13 | convolution fusion | flops 16941056 | bytes 352256 | tf_op jit(solution)/shard_map/sptbcr,srpkq->tbkqc/dot_general | solution.py:83
  51.2 0.1 maximum_maximum_fusion.1
  51.4 0.7 maximum_bitcast_fusion.1
  52.0 4.5 %all-to-all-done.2 = bf16[16,4,4,512]{3,2,1,0:T(4,128)(2,1)} async-done(((bf16[16,4,4,512]{3,2,1,0:T(4,128)(2,1)}), bf16[16,4,4,512]{3,2,1,0:T(4,128)(2,1)}, u32[]{:S(2)}, u32[]{:S(2)}) %all-to-all-start.2) | async-done | bytes 262176 | tf_op jit(solution)/shard_map/all_to_all | solution.py:76
  56.5 1.9 %copy.60 = bf16[16,4,4,512]{0,3,2,1:T(8,128)(2,1)S(1)} copy(bf16[16,4,4,512]{3,2,1,0:T(4,128)(2,1)} %all-to-all-done.2) | data formatting | bytes 524288 | tf_op jit(solution)/shard_map/all_to_all | solution.py:76
  58.5 1.8 %copy.61 = bf16[16,2,2,4,64,8]{4,0,5,1,3,2:T(8,128)(2,1)} copy(bf16[16,2,2,4,64,8]{0,5,4,3,2,1:T(8,128)(2,1)S(1)} %bitcast.84) | data formatting | bytes 524288 | tf_op jit(solution)/shard_map/reshape | solution.py:82
  60.3 1.0 maximum_bitcast_fusion
  61.2 0.3 copy.79
  61.5 0.1 reshape.184
  61.7 0.0 copy-done
  61.7 0.8 fusion.10
  62.5 1.1 fusion.6
  63.6 2.1 %copy.55 = bf16[16,2,2,4,64,8]{0,5,4,3,2,1:T(8,128)(2,1)S(1)} copy(bf16[16,2,2,4,64,8]{4,0,3,2,1,5:T(8,128)(2,1)} %fusion.6) | data formatting | bytes 524288 | tf_op jit(solution)/shard_map/convert_element_type | solution.py:111
  65.7 1.6 %copy.56 = bf16[16,4,4,512]{3,2,1,0:T(4,128)(2,1)} copy(bf16[16,4,4,512]{0,3,2,1:T(8,128)(2,1)S(1)} %bitcast.85) | data formatting | bytes 524288 | tf_op jit(solution)/shard_map/reshape | solution.py:111
  67.3 6.0 %all-to-all-start.1 = ((bf16[16,4,4,512]{3,2,1,0:T(4,128)(2,1)}), bf16[16,4,4,512]{3,2,1,0:T(4,128)(2,1)S(1)}, u32[]{:S(2)}, u32[]{:S(2)}) async-start(bf16[16,4,4,512]{3,2,1,0:T(4,128)(2,1)} %copy.56), calls=%async_computation.1 | async-start | bytes 524288 | tf_op jit(solution)/shard_map/all_to_all | solution.py:114
  73.3 1.3 %fusion.9 = bf16[2,4,32,2,64]{4,2,1,0,3:T(8,128)(2,1)S(1)} fusion(bf16[16,2,2,4,64,8]{4,0,5,1,3,2:T(8,128)(2,1)} %copy.61, bf16[16,8,1,32,1]{3,0,1,2,4:T(8,128)(2,1)S(1)} %get-tuple-element.9, bf16[16,8,1,32,1]{3,0,1,2,4:T(8,128)(2,1)S(1)} %get-tuple-element.8, bf16[16,8,1,32,1]{3,0,1,2,4:T(8,128)(2,1)S(1)} %fusion.34), kind=kOutput, calls=%fused_computation.15 | convolution fusion | flops 16941056 | bytes 352256 | tf_op jit(solution)/shard_map/sptbcr,srpkq->tbkqc/dot_general | solution.py:83
  74.6 0.5 bitcast_convert_fusion
  75.2 2.1 %copy.64 = bf16[32,2,2,32,128]{4,1,3,2,0:T(2,128)(2,1)} copy(bf16[32,2,2,32,128]{4,1,0,3,2:T(2,128)(2,1)S(1)} %bitcast.86) | data formatting | bytes 2097152 | tf_op jit(solution)/shard_map/reshape | solution.py:11
  77.3 5.4 %all-to-all-done.1 = bf16[16,4,4,512]{3,2,1,0:T(4,128)(2,1)S(1)} async-done(((bf16[16,4,4,512]{3,2,1,0:T(4,128)(2,1)}), bf16[16,4,4,512]{3,2,1,0:T(4,128)(2,1)S(1)}, u32[]{:S(2)}, u32[]{:S(2)}) %all-to-all-start.1) | async-done | bytes 262176 | tf_op jit(solution)/shard_map/all_to_all | solution.py:114
  82.7 10.7 %all-to-all-start.3 = ((bf16[32,2,2,32,128]{4,1,3,2,0:T(2,128)(2,1)}), bf16[32,2,2,32,128]{4,1,3,2,0:T(2,128)(2,1)S(1)}, u32[]{:S(2)}, u32[]{:S(2)}) async-start(bf16[32,2,2,32,128]{4,1,3,2,0:T(2,128)(2,1)} %copy.64), calls=%async_computation.3 | async-start | bytes 2097152 | tf_op jit(solution)/shard_map/all_to_all | solution.py:16
  93.4 5.8 %reshape.168 = bf16[64,4,64,8]{3,2,1,0:T(8,128)(2,1)} reshape(bf16[16,4,4,512]{3,2,1,0:T(4,128)(2,1)S(1)} %all-to-all-done.1) | data formatting | bytes 524288 | tf_op jit(solution)/shard_map/reshape | solution.py:116
  99.2 5.8 %fusion.2 = bf16[4,64,8,256]{3,2,1,0:T(8,128)(2,1)} fusion(bf16[64,4,64,8]{3,2,1,0:T(8,128)(2,1)} %reshape.168, bf16[256,64,1,1]{0,1,2,3:T(8,128)(2,1)S(1)} %reshape.172), kind=kOutput, calls=%fused_computation.4 | convolution fusion | flops 67633152 | bytes 1343488 | tf_op jit(solution)/shard_map/sbcr,ys->bcry/dot_general | solution.py:117
  105.0 14.9 %all-to-all-done.3 = bf16[32,2,2,32,128]{4,1,3,2,0:T(2,128)(2,1)S(1)} async-done(((bf16[32,2,2,32,128]{4,1,3,2,0:T(2,128)(2,1)}), bf16[32,2,2,32,128]{4,1,3,2,0:T(2,128)(2,1)S(1)}, u32[]{:S(2)}, u32[]{:S(2)}) %all-to-all-start.3) | async-done | bytes 1048608 | tf_op jit(solution)/shard_map/all_to_all | solution.py:16
  119.9 0.7 convert_reduce_fusion
  (7 shorter events, 0.1 us)
Async XLA Ops:
  0.6 61.0 %copy-start = (bf16[64,2,32,128]{3,2,1,0:T(8,128)(2,1)S(1)}, bf16[64,2,32,128]{3,2,1,0:T(8,128)(2,1)}, u32[]{:S(2)}) copy-start(bf16[64,2,32,128]{3,2,1,0:T(8,128)(2,1)} %param.5) | copy-start | bytes 3145732
  2.9 23.5 %copy-start.1 = (bf16[4,64,8,256]{3,2,1,0:T(8,128)(2,1)S(1)}, bf16[4,64,8,256]{3,2,1,0:T(8,128)(2,1)}, u32[]{:S(2)}) copy-start(bf16[4,64,8,256]{3,2,1,0:T(8,128)(2,1)} %param.3) | copy-start | bytes 3145732
  13.0 24.9 %all-to-all-start = ((bf16[16,4,4,512]{3,2,1,0:T(4,128)(2,1)}), bf16[16,4,4,512]{3,2,1,0:T(4,128)(2,1)S(1)}, u32[]{:S(2)}, u32[]{:S(2)}) async-start(bf16[16,4,4,512]{3,2,1,0:T(4,128)(2,1)} %reshape.164), calls=%async_computation | async-start | bytes 524288 | tf_op jit(solution)/shard_map/all_to_all | solution.py:77
  37.9 18.6 %all-to-all-start.2 = ((bf16[16,4,4,512]{3,2,1,0:T(4,128)(2,1)}), bf16[16,4,4,512]{3,2,1,0:T(4,128)(2,1)}, u32[]{:S(2)}, u32[]{:S(2)}) async-start(bf16[16,4,4,512]{3,2,1,0:T(4,128)(2,1)} %reshape.169), calls=%async_computation.2 | async-start | bytes 524288 | tf_op jit(solution)/shard_map/all_to_all | solution.py:76
  67.3 15.4 %all-to-all-start.1 = ((bf16[16,4,4,512]{3,2,1,0:T(4,128)(2,1)}), bf16[16,4,4,512]{3,2,1,0:T(4,128)(2,1)S(1)}, u32[]{:S(2)}, u32[]{:S(2)}) async-start(bf16[16,4,4,512]{3,2,1,0:T(4,128)(2,1)} %copy.56), calls=%async_computation.1 | async-start | bytes 524288 | tf_op jit(solution)/shard_map/all_to_all | solution.py:114
  82.7 37.2 %all-to-all-start.3 = ((bf16[32,2,2,32,128]{4,1,3,2,0:T(2,128)(2,1)}), bf16[32,2,2,32,128]{4,1,3,2,0:T(2,128)(2,1)S(1)}, u32[]{:S(2)}, u32[]{:S(2)}) async-start(bf16[32,2,2,32,128]{4,1,3,2,0:T(2,128)(2,1)} %copy.64), calls=%async_computation.3 | async-start | bytes 2097152 | tf_op jit(solution)/shard_map/all_to_all | solution.py:16
where the time goes:
time: 123 us; the launch traced here: 121 us
  starting transfers between devices  39.2 us (32%)
  local copies, waits for them, and re-layouts  39 us (32%)
  waiting for transfers between devices  24.8 us (20%)
  matrix products  13.3 us (11%)
  other arithmetic  3.47 us (3%)
    all_to_all x1, waiting for transfers between devices, summed_on_arrival(): tiles = lax.all_to_all(in_blocks(array, dim, size), axis, 0, 0, tiled=True)  14.9 us
    reshape x2, local copies, waits for them, and re-layouts, to_modes(): return along.reshape(slabs, 2 * modes_here, samples, channels * rows_here)  13.8 us
    all_to_all x1, starting transfers between devices, body(): lax.all_to_all(to_modes(cotangent), 'slab', split_axis=0, concat_axis=0,...  13.4 us
    all_to_all x1, starting transfers between devices, summed_on_arrival(): tiles = lax.all_to_all(in_blocks(array, dim, size), axis, 0, 0, tiled=True)  10.7 us
    all_to_all x1, starting transfers between devices, body(): lax.all_to_all(to_modes(activation), 'slab', split_axis=0, concat_axis=0,...  9.12 us
    convert_element_type x2, local copies, waits for them, and re-layouts, to_modes(): along = along.astype(jnp.bfloat16)  6.44 us
    all_to_all x1, starting transfers between devices, body(): lax.all_to_all(spread, 'slab', split_axis=0, concat_axis=0, tiled=True)  6.02 us
    reshape x1, local copies, waits for them, and re-layouts, body(): lines = member.reshape(2 * modes_y, amount, channels, rows_here)  5.83 us
  transfers between devices with their start and end apart: 4, of which 3 were waited for; matrix products, arithmetic and copies ran while one was open for 26% of the time, Pallas kernels for 0%

commit v1 on v0

v1 whole, which is shorter than its diff:
```python
import functools

import jax
import jax.numpy as jnp
import numpy as np
from jax import lax
from jax.experimental import pallas as pl
from jax.experimental.pallas import tpu as pltpu
from jax.sharding import PartitionSpec as P

MESH = pl.DeviceIdType.MESH
F32 = jnp.float32
BF16 = jnp.bfloat16


def retained(length, modes):
    index = np.arange(modes)
    return np.where(index < modes // 2, index, index + (length - modes))


def cos_sin(length, modes):
    phase = np.arange(length)[:, None] * retained(length, modes)[None, :] % length
    angle = phase * (2.0 * np.pi / length)
    factor = 1.0 / np.sqrt(length)
    return np.cos(angle) * factor, np.sin(angle) * factor


def tables(slabs):
    cos_y, sin_y = cos_sin(128, 32)
    table_y = np.concatenate(
        [np.concatenate([cos_y, -sin_y], 1), np.concatenate([sin_y, cos_y], 1)], 0
    )
    ty = table_y.reshape(256, 2, slabs, 32 // slabs).transpose(2, 3, 1, 0).reshape(64, 256)
    cos_x, sin_x = cos_sin(128, 32)
    table_x = np.stack(
        [np.stack([cos_x, -sin_x], 2), np.stack([sin_x, cos_x], 2)], 1
    )
    fx = table_x.reshape(slabs, 128 // slabs, 2, 32, 2).transpose(4, 3, 0, 2, 1).reshape(64, 256)
    return jnp.asarray(ty, BF16), jnp.asarray(fx, BF16), jnp.asarray(fx.T.copy(), BF16)


def ring(step):
    return 4 + (1 - 2 * lax.rem(step, 2)) * lax.div(step + 1, 2)


def slab_peer(me, step):
    across = lax.rem(lax.div(me, 8) + 1 - lax.rem(step, 2), 2)
    return across * 8 + lax.rem(lax.rem(me, 8) + ring(lax.div(step, 2)), 8)


def dp_peer(me, step):
    sub = lax.rem(step, 4)
    core = lax.rem(lax.rem(me, 2) + 1 - lax.rem(sub, 2), 2)
    across = lax.rem(lax.div(me, 16) + 1 - lax.div(sub, 2), 2)
    along = lax.rem(lax.rem(lax.div(me, 2), 8) + ring(lax.div(step, 4)), 8)
    return (across * 8 + along) * 2 + core


def nt(a, b):
    return lax.dot_general(a, b, (((1,), (1,)), ((), ())), preferred_element_type=F32)


def tn(a, b):
    return lax.dot_general(a, b, (((0,), (0,)), ((), ())), preferred_element_type=F32)


def kernel(
    slabs, groups,
    act_hbm, cot_hbm, w_hbm, ty_ref, fx_ref, tx_ref,
    grad_ref, wgrad_ref,
    act_v, cot_v, w_v, wm, lines, folded,
    send_a, send_c, got_a, got_c, send_e, got_e,
    spectra, pair_a, pair_c, all_a, all_c, stacked, mixed, sums, wsend,
    load_sem, send_sem, recv_sem,
):
    me_s = lax.axis_index("slab")
    me_d = lax.axis_index("dp")

    loads = [
        pltpu.make_async_copy(src, dst, load_sem.at[n])
        for n, (src, dst) in enumerate(((cot_hbm, cot_v), (act_hbm, act_v), (w_hbm, w_v)))
    ]
    for load in loads:
        load.start()

    barrier = pltpu.get_barrier_semaphore()

    @pl.loop(0, slabs - 1)
    def _(step):
        pl.semaphore_signal(
            barrier, inc=1, device_id={"slab": slab_peer(me_s, step)}, device_id_type=MESH
        )

    @pl.loop(0, groups - 1)
    def _(step):
        pl.semaphore_signal(
            barrier, inc=1, device_id={"dp": dp_peer(me_d, step)}, device_id_type=MESH
        )

    def exchange(axis, me, peer_of, count, src, dst, n):
        @pl.loop(0, count - 1)
        def _(step):
            peer = peer_of(me, step)
            pltpu.make_async_remote_copy(
                src_ref=src.at[peer], dst_ref=dst.at[me], send_sem=send_sem.at[n],
                recv_sem=recv_sem.at[n], device_id={axis: peer}, device_id_type=MESH,
            ).start()

    def wait_all(ref, count, sem):
        part = ref.at[pl.ds(0, count - 1)]
        pltpu.make_async_copy(part, part, sem).wait()

    over_slab = functools.partial(exchange, "slab", me_s, slab_peer, slabs)
    over_dp = functools.partial(exchange, "dp", me_d, dp_peer, groups)

    def along_y(field, send):
        for c in range(8):
            part = field[c * 32 : (c + 1) * 32].astype(F32).reshape(256, 256)
            for half in range(2):
                lines[half, c * 256 : (c + 1) * 256, :] = part[:, half * 128 : half * 128 + 128]
        for r in range(8):
            rows = jnp.concatenate(
                [lines[half, pl.ds(r, 256, stride=8), :] for half in range(2)], axis=1
            ).astype(BF16)
            moved = nt(ty_ref[...], rows)
            for half in range(2):
                folded[half, pl.ds(r, 64, stride=8), :] = moved[:, half * 128 : half * 128 + 128]
        for half in range(2):
            send[:, :, :, half * 128 : half * 128 + 128] = (
                folded[half].astype(BF16).reshape(slabs, 2, 16, 128)
            )

    loads[0].wait()
    along_y(cot_v, send_c)
    got_c[me_s] = send_c[me_s]
    pl.semaphore_wait(barrier, slabs + groups - 2)
    over_slab(send_c, got_c, 0)
    loads[1].wait()
    along_y(act_v, send_a)
    got_a[me_s] = send_a[me_s]
    over_slab(send_a, got_a, 1)

    loads[2].wait()
    for c in range(8):
        part = w_v[c * 8 : (c + 1) * 8].astype(F32).reshape(512, 128)
        lines[c // 4, c % 4 * 512 : (c % 4 + 1) * 512, :] = part

    @pl.loop(0, 64)
    def _(m):
        for half in range(2):
            wm[m, half * 32 : half * 32 + 32, :] = lines[
                half, pl.ds(m, 32, stride=64), :
            ].astype(BF16)

    lane = lax.broadcasted_iota(jnp.int32, (32, 128), 1)
    low = lane < 64

    def spec_of(got):
        return [
            jnp.dot(fx_ref[...], got[:, t].reshape(256, 256), preferred_element_type=F32)
            .astype(BF16)
            .astype(F32)
            for t in range(2)
        ]

    def to_pair(specs, pair):
        for t in range(2):
            for q in range(2):
                for h in range(2):
                    spectra[pl.ds(t * 128 + q * 2 + h, 32, stride=4), :] = specs[t][
                        q * 32 : q * 32 + 32, h * 128 : h * 128 + 128
                    ]
        pair[...] = spectra[...].astype(BF16).reshape(groups, 256 // groups, 128)

    wait_all(got_c, slabs, recv_sem.at[0])
    specs = spec_of(got_c)

    for t in range(2):
        for h in range(2):
            re = specs[t][0:32, h * 128 : h * 128 + 128]
            im = specs[t][32:64, h * 128 : h * 128 + 128]
            re_r = pltpu.roll(re, 64, 1)
            im_r = pltpu.roll(im, 64, 1)
            rows = (
                jnp.where(low, re, im_r),
                jnp.where(low, im, -re_r),
                jnp.where(low, re_r, im),
                jnp.where(low, im_r, -re),
            )
            for n, row in enumerate(rows):
                stacked[pl.ds(t * 256 + h * 4 + n, 32, stride=8), :] = row

    @pl.loop(0, 32)
    def _(n):
        both = nt(
            stacked[pl.ds(pl.multiple_of(n * 16, 16), 16), :].astype(BF16),
            wm[pl.ds(n * 2, 2)].reshape(128, 128),
        )
        turned = pltpu.roll(both, 64, 1)
        mixed[pl.ds(pl.multiple_of(n * 16, 16), 8), :] = both[0:8]
        mixed[pl.ds(pl.multiple_of(n * 16 + 8, 8), 8), :] = turned[8:16]

    for t in range(2):
        rows = []
        for q in range(2):
            tiles = []
            for h in range(2):
                first = mixed[pl.ds(t * 256 + h * 4 + q, 32, stride=8), :]
                second = mixed[pl.ds(t * 256 + h * 4 + 2 + q, 32, stride=8), :]
                tiles.append(jnp.where(low, first, pltpu.roll(second, 64, 1)))
            rows.append(jnp.concatenate(tiles, axis=1))
        grads = jnp.concatenate(rows, axis=0).astype(BF16)
        spread = jnp.dot(tx_ref[...], grads, preferred_element_type=F32)
        send_e[:, t] = spread.astype(BF16).reshape(slabs, 16, 256)
    got_e[me_s] = send_e[me_s]
    over_slab(send_e, got_e, 2)

    to_pair(specs, pair_c)
    all_c[me_d] = pair_c[me_d]
    over_dp(pair_c, all_c, 3)

    wait_all(got_a, slabs, recv_sem.at[1])
    to_pair(spec_of(got_a), pair_a)
    all_a[me_d] = pair_a[me_d]
    over_dp(pair_a, all_a, 4)

    wait_all(all_c, groups, recv_sem.at[3])
    wait_all(all_a, groups, recv_sem.at[4])
    sums[0] = all_a[...].astype(F32).reshape(256, 128)
    sums[1] = all_c[...].astype(F32).reshape(256, 128)
    wide = lax.broadcasted_iota(jnp.int32, (64, 128), 1) < 64
    for m in range(2):
        def part(which, q):
            return jnp.concatenate(
                [sums[which, pl.ds(m * 4 + q * 2 + h, groups, stride=8), :] for h in range(2)],
                axis=0,
            )

        ins = jnp.concatenate([part(0, 0), part(0, 1)], axis=0).astype(BF16)
        out_re, out_im = part(1, 0), part(1, 1)
        outs = jnp.concatenate([out_re, out_im], axis=0)
        swapped = jnp.concatenate([out_im, -out_re], axis=0)
        prod = tn(ins, jnp.concatenate([outs, swapped], axis=1).astype(BF16))
        top, bottom = prod[0:64], prod[64:128]
        total = jnp.where(
            wide,
            top[:, 0:128] + pltpu.roll(bottom[:, 0:128], 64, 1),
            pltpu.roll(top[:, 128:256], 64, 1) + bottom[:, 128:256],
        )
        mixed[m * 64 : m * 64 + 64, :] = total
    for m in range(2):
        for i in range(2):
            wsend[:, i, m, :] = mixed[pl.ds(m * 64 + i, groups, stride=2), :]
    wgrad_ref[me_d] = wsend[me_d]
    over_dp(wsend, wgrad_ref, 5)

    wait_all(got_e, slabs, recv_sem.at[2])
    for half in range(2):
        folded[half] = got_e[:, :, :, half * 128 : half * 128 + 128].astype(F32).reshape(512, 128)
    for r in range(8):
        rows = jnp.concatenate(
            [folded[half, pl.ds(r, 64, stride=8), :] for half in range(2)], axis=1
        ).astype(BF16)
        values = tn(rows, ty_ref[...])
        for half in range(2):
            lines[half, pl.ds(r, 256, stride=8), :] = values[:, half * 128 : half * 128 + 128]
    for c in range(8):
        grad_ref[c * 32 : (c + 1) * 32] = (
            jnp.concatenate(
                [lines[half, c * 256 : (c + 1) * 256, :] for half in range(2)], axis=1
            )
            .astype(BF16)
            .reshape(32, 8, 256)
        )

    wait_all(wgrad_ref, groups, recv_sem.at[5])
    for n, ref in enumerate((send_c, send_a, send_e)):
        wait_all(ref, slabs, send_sem.at[n])
    for n, ref in enumerate((pair_c, pair_a, wsend)):
        wait_all(ref, groups, send_sem.at[3 + n])


def body(activation, cotangent, spectral_weight, slabs, groups):
    ty, fx, tx = tables(slabs)
    vmem = pl.BlockSpec(memory_space=pltpu.VMEM)
    hbm = pl.BlockSpec(memory_space=pl.ANY)
    block = (slabs, 2, 16, 256)
    pair = (groups, 256 // groups, 128)
    grad, wgrad = pl.pallas_call(
        functools.partial(kernel, slabs, groups),
        out_shape=(
            jax.ShapeDtypeStruct((256, 8, 256), BF16),
            jax.ShapeDtypeStruct((groups, 2, 2, 128), F32),
        ),
        in_specs=[hbm] * 3 + [vmem] * 3,
        out_specs=[vmem, vmem],
        scratch_shapes=[
            pltpu.VMEM((256, 8, 256), BF16),
            pltpu.VMEM((256, 8, 256), BF16),
            pltpu.VMEM((64, 64, 128), BF16),
            pltpu.VMEM((64, 64, 128), BF16),
            pltpu.VMEM((2, 2048, 128), F32),
            pltpu.VMEM((2, 512, 128), F32),
        ]
        + [pltpu.VMEM(block, BF16)] * 6
        + [pltpu.VMEM((256, 128), F32)]
        + [pltpu.VMEM(pair, BF16)] * 4
        + [
            pltpu.VMEM((512, 128), F32),
            pltpu.VMEM((512, 128), F32),
            pltpu.VMEM((2, 256, 128), F32),
            pltpu.VMEM((groups, 2, 2, 128), F32),
            pltpu.SemaphoreType.DMA((3,)),
            pltpu.SemaphoreType.DMA((6,)),
            pltpu.SemaphoreType.DMA((6,)),
        ],
        compiler_params=pltpu.CompilerParams(collective_id=0, has_side_effects=True),
    )(
        activation.reshape(256, 8, 256),
        cotangent.reshape(256, 8, 256),
        spectral_weight.reshape(64, 64, 128),
        ty,
        fx,
        tx,
    )
    wgrad = wgrad.transpose(1, 0, 2, 3).reshape(2, 2, 32, 128)
    return grad.reshape(4, 64, 8, 256), wgrad


def solution(mesh):
    placed = (P("dp", None, "slab", None), P("dp", None, "slab", None), P(None, "slab", None, None))
    return jax.shard_map(
        functools.partial(body, slabs=mesh.shape["slab"], groups=mesh.shape["dp"]),
        mesh=mesh,
        in_specs=placed,
        out_specs=(P("dp", None, "slab", None), P("dp", "slab", None, None)),
        check_vma=False,
    )
```

time: 123 us -> 52.6 us (0.43); the launches traced: 121 us -> 52.3 us
  Pallas kernels: 0 us -> 47.9 us
  starting transfers between devices: 39.2 us -> 0 us
  local copies, waits for them, and re-layouts: 39 us -> 3.75 us
  waiting for transfers between devices: 24.8 us -> 0 us
  matrix products: 13.3 us -> 0 us
  other arithmetic: 3.47 us -> 0 us
    pallas_call x0 -> x1, Pallas kernels: none -> 47.9 us  [body(): pl.pallas_call(functools.partial(kernel, slabs, groups), out_shape=(jax.S...]
    all_to_all x4 -> x0, starting transfers between devices: 39.2 us -> none  [the longest x1 13.4 us: body(): lax.all_to_all(to_modes(cotangent), 'slab', split_axis=0, concat_axis=0,...]
    reshape x11 -> x0, local copies, waits for them, and re-layouts: 27.4 us -> none  [the longest x2 13.8 us: to_modes(): return along.reshape(slabs, 2 * modes_here, samples, channels * rows_here)]
    all_to_all x4 -> x0, waiting for transfers between devices: 24.8 us -> none  [the longest x1 14.9 us: summed_on_arrival(): tiles = lax.all_to_all(in_blocks(array, dim, size), axis, 0, 0, tiled=True)]
    dot_general x8 -> x0, matrix products: 13.3 us -> none  [the longest x1 5.78 us: body(): jnp.einsum('sbcr,ys->bcry', lines, table_y, preferred_element_type=jnp.fl...]
    convert_element_type x3 -> x0, local copies, waits for them, and re-layouts: 8.53 us -> none  [the longest x2 6.44 us: to_modes(): along = along.astype(jnp.bfloat16)]
    all_to_all x2 -> x0, local copies, waits for them, and re-layouts: 3.01 us -> none  [the longest x1 1.94 us: body(): lax.all_to_all(to_modes(activation), 'slab', split_axis=0, concat_axis=0,...]
    unnamed x4 -> x1, local copies, waits for them, and re-layouts: 0.01 us -> 2.26 us
  transfers between devices with their start and end apart: 4 -> 0, of which waited for: 3 -> 0; matrix products, arithmetic and copies ran while one was open for 26% -> 0% of each run, Pallas kernels for 0% -> 0%
where the time goes in v1:
time: 52.6 us; the launch traced here: 52.3 us
  Pallas kernels  47.9 us (91%)
  local copies, waits for them, and re-layouts  3.75 us (7%)
  between operations  0.64 us (1%)
    pallas_call x1, Pallas kernels, body(): pl.pallas_call(functools.partial(kernel, slabs, groups), out_shape=(jax.S...  47.9 us
    unnamed x1, local copies, waits for them, and re-layouts  2.26 us
    transpose x1, local copies, waits for them, and re-layouts, body(): wgrad = wgrad.transpose(1, 0, 2, 3).reshape(2, 2, 32, 128)  1.49 us

profile of v1, /device:TPU:1, one launch (start us, length us, event | category | flops | bytes accessed | tf_op | source)
XLA Modules:
  0.0 52.3 jit_solution(12056257729950149083)
XLA Ops:
  0.6 47.9 %shard_map.77 = (bf16[256,8,256]{2,1,0:T(8,128)(2,1)}, f32[32,2,2,128]{3,2,1,0:T(2,128)}) custom-call(bf16[256,8,256]{2,1,0:T(8,128)(2,1)} %bitcast.6, bf16[256,8,256]{2,1,0:T(8,128)(2,1)} %bitcast.7, bf16[64,64,128]{2,1,0:T(8,128)(2,1)} %bitcast.8, bf16[64,256]{1,0:T(8,128)(2,1)} %constant.6.clone.ty_ref, bf16[64,256]{1,0:T(8,128)(2,1)} %constant.7.clone.fx_ref, ...), custom_call_target="tpu_custom_call" | custom-call | tf_op jit(solution)/shard_map/pallas_call | solution.py:289
  48.6 1.5 %copy.8 = f32[2,32,2,128]{3,2,1,0:T(2,128)} copy(f32[2,32,2,128]{3,2,0,1:T(2,128)} %bitcast.11) | data formatting | bytes 131072 | tf_op jit(solution)/shard_map/transpose | solution.py:326
  50.1 2.3 %copy.10 = bf16[4,64,8,256]{3,2,1,0:T(8,128)(2,1)} copy(bf16[4,64,8,256]{3,2,1,0:T(8,128)(2,1)} %bitcast.9) | data formatting | bytes 2097152

commit v2 on v1

v2 whole, which is shorter than its diff:
```python
import functools

import jax
import jax.numpy as jnp
import numpy as np
from jax import lax
from jax.experimental import pallas as pl
from jax.experimental.pallas import tpu as pltpu
from jax.sharding import PartitionSpec as P

MESH = pl.DeviceIdType.MESH
F32 = jnp.float32
BF16 = jnp.bfloat16


def retained(length, modes):
    index = np.arange(modes)
    return np.where(index < modes // 2, index, index + (length - modes))


def cos_sin(length, modes):
    phase = np.arange(length)[:, None] * retained(length, modes)[None, :] % length
    angle = phase * (2.0 * np.pi / length)
    factor = 1.0 / np.sqrt(length)
    return np.cos(angle) * factor, np.sin(angle) * factor


def tables(slabs):
    cos_y, sin_y = cos_sin(128, 32)
    table_y = np.concatenate(
        [np.concatenate([cos_y, -sin_y], 1), np.concatenate([sin_y, cos_y], 1)], 0
    )
    ty = table_y.reshape(256, 2, slabs, 32 // slabs).transpose(2, 3, 1, 0).reshape(64, 256)
    cos_x, sin_x = cos_sin(128, 32)
    table_x = np.stack(
        [np.stack([cos_x, -sin_x], 2), np.stack([sin_x, cos_x], 2)], 1
    )
    fx = table_x.reshape(slabs, 128 // slabs, 2, 32, 2).transpose(4, 3, 0, 2, 1).reshape(64, 256)
    packed = np.zeros((2048, 256), np.float32)
    packed[0:64], packed[64:128], packed[128:384, 0:64] = ty, fx, fx.T
    return jnp.asarray(ty, BF16), jnp.asarray(packed, BF16)


RING = (4, 3, 5, 2, 6, 1, 7, 0)


def slab_peers(me):
    part, along = lax.div(me, 8), lax.rem(me, 8)
    parts = [lax.rem(part + n, 2) * 8 for n in range(2)]
    peers = [parts[n] + lax.rem(along + off, 8) for off in RING for n in (1, 0)]
    return peers[:-1]


def dp_peers(me):
    part, along, core = lax.div(me, 16), lax.rem(lax.div(me, 2), 8), lax.rem(me, 2)
    parts = [lax.rem(part + n, 2) * 16 for n in range(2)]
    cores = [lax.rem(core + n, 2) for n in range(2)]
    peers = []
    for off in RING:
        row = lax.rem(along + off, 8) * 2
        peers += [row + parts[n] + cores[c] for n in (1, 0) for c in (1, 0)]
    return peers[:-1]


def nt(a, b):
    return lax.dot_general(a, b, (((1,), (1,)), ((), ())), preferred_element_type=F32)


def tn(a, b):
    return lax.dot_general(a, b, (((0,), (0,)), ((), ())), preferred_element_type=F32)


def kernel(
    slabs, groups,
    act_hbm, cot_hbm, w_hbm, tab_hbm,
    got_e, wgrad_ref,
    ty_ref, fx_ref, tx_ref, act_v, cot_v, w_v, wm, lines, folded,
    send_a, send_c, got_a, got_c, send_e,
    spectra, pair_a, pair_c, all_a, all_c, stacked, mixed, sums, wsend,
    load_sem, send_sem, recv_sem,
):
    me_s = lax.axis_index("slab")
    me_d = lax.axis_index("dp")

    loads = [
        pltpu.make_async_copy(src, dst, load_sem.at[n])
        for n, (src, dst) in enumerate(
            (
                (tab_hbm.at[pl.ds(0, 64)], ty_ref),
                (cot_hbm.at[pl.ds(0, 128)], cot_v.at[pl.ds(0, 128)]),
                (cot_hbm.at[pl.ds(128, 128)], cot_v.at[pl.ds(128, 128)]),
                (act_hbm, act_v), (w_hbm, w_v),
                (tab_hbm.at[pl.ds(64, 64)], fx_ref),
                (tab_hbm.at[pl.ds(128, 256), pl.ds(0, 128)], tx_ref),
            )
        )
    ]
    for load in loads:
        load.start()

    peers_s, peers_d = slab_peers(me_s), dp_peers(me_d)
    barrier = pltpu.get_barrier_semaphore()
    for axis, peers in (("slab", peers_s), ("dp", peers_d)):
        for peer in peers:
            pl.semaphore_signal(barrier, inc=1, device_id={axis: peer}, device_id_type=MESH)

    def exchange(axis, me, peers, src, dst, n, rank=0):
        lead = (slice(None),) * rank
        for peer in peers:
            pltpu.make_async_remote_copy(
                src_ref=src.at[(*lead, peer)], dst_ref=dst.at[(*lead, me)],
                send_sem=send_sem.at[n], recv_sem=recv_sem.at[n],
                device_id={axis: peer}, device_id_type=MESH,
            ).start()

    def wait_all(ref, count, sem):
        part = ref.at[pl.ds(0, count - 1)] if ref.shape[0] == count else ref.at[:, pl.ds(0, count - 1)]
        pltpu.make_async_copy(part, part, sem).wait()

    over_slab = functools.partial(exchange, "slab", me_s, peers_s)
    over_dp = functools.partial(exchange, "dp", me_d, peers_d)

    def along_y(field, send, h):
        for c in range(4):
            part = field[h * 128 + c * 32 : h * 128 + (c + 1) * 32].astype(F32).reshape(256, 256)
            for half in range(2):
                lines[half, c * 256 : (c + 1) * 256, :] = part[:, half * 128 : half * 128 + 128]
        for r in range(8):
            rows = jnp.concatenate(
                [lines[half, pl.ds(r, 128, stride=8), :] for half in range(2)], axis=1
            ).astype(BF16)
            folded[pl.ds(r, 64, stride=8), :] = nt(ty_ref[...], rows)
        send[h] = folded[...].astype(BF16).reshape(slabs, 2, 16, 128)

    loads[0].wait()
    loads[1].wait()
    along_y(cot_v, send_c, 0)
    pl.semaphore_wait(barrier, slabs + groups - 2)
    over_slab(send_c.at[0], got_c.at[0], 0)
    loads[2].wait()
    along_y(cot_v, send_c, 1)
    over_slab(send_c.at[1], got_c.at[1], 1)
    for h in range(2):
        got_c[h, me_s] = send_c[h, me_s]
    loads[3].wait()
    along_y(act_v, send_a, 0)
    along_y(act_v, send_a, 1)
    over_slab(send_a, got_a, 2, rank=1)
    for h in range(2):
        got_a[h, me_s] = send_a[h, me_s]

    loads[4].wait()
    for c in range(8):
        part = w_v[c * 8 : (c + 1) * 8].astype(F32).reshape(512, 128)
        lines[c // 4, c % 4 * 512 : (c % 4 + 1) * 512, :] = part

    @pl.loop(0, 64)
    def _(m):
        for half in range(2):
            wm[m, half * 32 : half * 32 + 32, :] = lines[
                half, pl.ds(m, 32, stride=64), :
            ].astype(BF16)

    lane = lax.broadcasted_iota(jnp.int32, (32, 128), 1)
    low = lane < 64

    def spec_of(got):
        return [
            [
                jnp.dot(fx_ref[...], got[h, :, t].reshape(256, 128), preferred_element_type=F32)
                .astype(BF16)
                .astype(F32)
                for h in range(2)
            ]
            for t in range(2)
        ]

    def to_pair(specs, pair):
        for t in range(2):
            for q in range(2):
                for h in range(2):
                    spectra[pl.ds(t * 128 + q * 2 + h, 32, stride=4), :] = specs[t][h][
                        q * 32 : q * 32 + 32
                    ]
        pair[...] = spectra[...].astype(BF16).reshape(groups, 256 // groups, 128)

    wait_all(got_c.at[0], slabs, recv_sem.at[0])
    wait_all(got_c.at[1], slabs, recv_sem.at[1])
    loads[5].wait()
    loads[6].wait()
    specs = spec_of(got_c)

    for t in range(2):
        for h in range(2):
            re, im = specs[t][h][0:32], specs[t][h][32:64]
            re_r = pltpu.roll(re, 64, 1)
            im_r = pltpu.roll(im, 64, 1)
            rows = (
                jnp.where(low, re, im_r),
                jnp.where(low, im, -re_r),
                jnp.where(low, re_r, im),
                jnp.where(low, im_r, -re),
            )
            for n, row in enumerate(rows):
                stacked[pl.ds(t * 256 + h * 4 + n, 32, stride=8), :] = row

    for n in range(16):
        both = nt(
            stacked[n * 32 : n * 32 + 32, :].astype(BF16),
            wm[n * 4 : n * 4 + 4].reshape(256, 128),
        )
        for m in range(4):
            block = both[m * 8 : m * 8 + 8, m // 2 * 128 : m // 2 * 128 + 128]
            mixed[n * 32 + m * 8 : n * 32 + m * 8 + 8, :] = (
                pltpu.roll(block, 64, 1) if m % 2 else block
            )

    for t in range(2):
        rows = []
        for q in range(2):
            tiles = []
            for h in range(2):
                first = mixed[pl.ds(t * 256 + h * 4 + q, 32, stride=8), :]
                second = mixed[pl.ds(t * 256 + h * 4 + 2 + q, 32, stride=8), :]
                tiles.append(jnp.where(low, first, pltpu.roll(second, 64, 1)))
            rows.append(jnp.concatenate(tiles, axis=1))
        grads = jnp.concatenate(rows, axis=0).astype(BF16)
        spread = jnp.dot(tx_ref[:, 0:64], grads, preferred_element_type=F32)
        for h in range(2):
            send_e[h, :, t] = (
                spread[:, h * 128 : h * 128 + 128].astype(BF16).reshape(slabs, 16, 128)
            )
    for h in range(2):
        got_e[h, me_s] = send_e[h, me_s]
    over_slab(send_e, got_e, 3, rank=1)

    to_pair(specs, pair_c)
    all_c[me_d] = pair_c[me_d]
    over_dp(pair_c, all_c, 4)

    wait_all(got_a, slabs, recv_sem.at[2])
    to_pair(spec_of(got_a), pair_a)
    all_a[me_d] = pair_a[me_d]
    over_dp(pair_a, all_a, 5)

    wait_all(all_c, groups, recv_sem.at[4])
    wait_all(all_a, groups, recv_sem.at[5])
    sums[0] = all_a[...].astype(F32).reshape(256, 128)
    sums[1] = all_c[...].astype(F32).reshape(256, 128)
    wide = lax.broadcasted_iota(jnp.int32, (64, 128), 1) < 64
    for m in range(2):
        def part(which, q):
            return jnp.concatenate(
                [sums[which, pl.ds(m * 4 + q * 2 + h, groups, stride=8), :] for h in range(2)],
                axis=0,
            )

        ins = jnp.concatenate([part(0, 0), part(0, 1)], axis=0).astype(BF16)
        out_re, out_im = part(1, 0), part(1, 1)
        outs = jnp.concatenate([out_re, out_im], axis=0)
        swapped = jnp.concatenate([out_im, -out_re], axis=0)
        prod = tn(ins, jnp.concatenate([outs, swapped], axis=1).astype(BF16))
        top, bottom = prod[0:64], prod[64:128]
        total = jnp.where(
            wide,
            top[:, 0:128] + pltpu.roll(bottom[:, 0:128], 64, 1),
            pltpu.roll(top[:, 128:256], 64, 1) + bottom[:, 128:256],
        )
        mixed[m * 64 : m * 64 + 64, :] = total
    for m in range(2):
        for i in range(2):
            wsend[i, :, m, :] = mixed[pl.ds(m * 64 + i, groups, stride=2), :]
    for i in range(2):
        wgrad_ref[i, me_d] = wsend[i, me_d]
    over_dp(wsend, wgrad_ref, 6, rank=1)

    wait_all(got_e, slabs, recv_sem.at[3])
    wait_all(wgrad_ref, groups, recv_sem.at[6])
    for n, ref in enumerate((send_c.at[0], send_c.at[1], send_a, send_e)):
        wait_all(ref, slabs, send_sem.at[n])
    for n, ref in enumerate((pair_c, pair_a, wsend)):
        wait_all(ref, groups, send_sem.at[4 + n])


def expand(got_ref, ty_ref, wgrad_ref, grad_hbm, wgrad_hbm, folded, lines, grad_v, sems):
    copies = [pltpu.make_async_copy(wgrad_ref, wgrad_hbm, sems.at[0])]
    copies[0].start()
    for h in range(2):
        folded[h] = got_ref[h].astype(F32).reshape(512, 128)
        for r in range(8):
            values = tn(folded[h, pl.ds(r, 64, stride=8), :].astype(BF16), ty_ref[...])
            for half in range(2):
                lines[h, half, pl.ds(r, 128, stride=8), :] = values[
                    :, half * 128 : half * 128 + 128
                ]
        for c in range(4):
            grad_v[h, c * 32 : (c + 1) * 32] = (
                jnp.concatenate(
                    [lines[h, half, c * 256 : (c + 1) * 256, :] for half in range(2)], axis=1
                )
                .astype(BF16)
                .reshape(32, 8, 256)
            )
        copies.append(
            pltpu.make_async_copy(
                grad_v.at[h], grad_hbm.at[pl.ds(h * 128, 128)], sems.at[h + 1]
            )
        )
        copies[-1].start()
    for copy in copies:
        copy.wait()


def body(activation, cotangent, spectral_weight, slabs, groups):
    ty, packed = tables(slabs)
    block = (2, slabs, 2, 16, 128)
    pair = (groups, 256 // groups, 128)
    total = (2, groups, 2, 128)
    got, wgrad = pl.pallas_call(
        functools.partial(kernel, slabs, groups),
        out_shape=(jax.ShapeDtypeStruct(block, BF16), jax.ShapeDtypeStruct(total, F32)),
        in_specs=[pl.BlockSpec(memory_space=pltpu.HBM)] * 4,
        out_specs=[pl.BlockSpec(memory_space=pltpu.VMEM)] * 2,
        scratch_shapes=[
            pltpu.VMEM((64, 256), BF16),
            pltpu.VMEM((64, 256), BF16),
            pltpu.VMEM((256, 128), BF16),
            pltpu.VMEM((256, 8, 256), BF16),
            pltpu.VMEM((256, 8, 256), BF16),
            pltpu.VMEM((64, 64, 128), BF16),
            pltpu.VMEM((64, 64, 128), BF16),
            pltpu.VMEM((2, 2048, 128), F32),
            pltpu.VMEM((512, 128), F32),
        ]
        + [pltpu.VMEM(block, BF16)] * 5
        + [pltpu.VMEM((256, 128), F32)]
        + [pltpu.VMEM(pair, BF16)] * 4
        + [
            pltpu.VMEM((512, 128), F32),
            pltpu.VMEM((512, 128), F32),
            pltpu.VMEM((2, 256, 128), F32),
            pltpu.VMEM(total, F32),
            pltpu.SemaphoreType.DMA((7,)),
            pltpu.SemaphoreType.DMA((7,)),
            pltpu.SemaphoreType.DMA((7,)),
        ],
        compiler_params=pltpu.CompilerParams(
            collective_id=0, has_side_effects=True, vmem_limit_bytes=67043328 - 11300000
        ),
    )(
        activation.reshape(256, 8, 256),
        cotangent.reshape(256, 8, 256),
        spectral_weight.reshape(64, 64, 128),
        packed,
    )
    grad, wgrad = pl.pallas_call(
        expand,
        out_shape=(jax.ShapeDtypeStruct((256, 8, 256), BF16), jax.ShapeDtypeStruct(total, F32)),
        in_specs=[pl.BlockSpec(memory_space=pltpu.VMEM)] * 3,
        out_specs=[pl.BlockSpec(memory_space=pltpu.HBM)] * 2,
        scratch_shapes=[
            pltpu.VMEM((2, 512, 128), F32),
            pltpu.VMEM((2, 2, 1024, 128), F32),
            pltpu.VMEM((2, 128, 8, 256), BF16),
            pltpu.SemaphoreType.DMA((3,)),
        ],
        compiler_params=pltpu.CompilerParams(vmem_limit_bytes=20 << 20),
    )(got, ty, wgrad)
    return grad.reshape(4, 64, 8, 256), wgrad.reshape(2, 2, 32, 128)


def solution(mesh):
    placed = (P("dp", None, "slab", None), P("dp", None, "slab", None), P(None, "slab", None, None))
    return jax.shard_map(
        functools.partial(body, slabs=mesh.shape["slab"], groups=mesh.shape["dp"]),
        mesh=mesh,
        in_specs=placed,
        out_specs=(P("dp", None, "slab", None), P("dp", "slab", None, None)),
        check_vma=False,
    )
```

time: 52.6 us -> 45 us (0.86)
  local copies, waits for them, and re-layouts: 3.75 us -> 0.01 us
  Pallas kernels: 47.9 us -> 44.2 us
    pallas_call x1, Pallas kernels: 47.9 us -> 42.7 us  [body(): pl.pallas_call(functools.partial(kernel, slabs, groups), out_shape=(jax.S...]
    unnamed x1 -> x2, local copies, waits for them, and re-layouts: 2.26 us -> 0.01 us
    pallas_call x0 -> x1, Pallas kernels: none -> 1.49 us  [body(): pl.pallas_call(expand, out_shape=(jax.ShapeDtypeStruct((256, 8, 256), BF1...]
    transpose x1 -> x0, local copies, waits for them, and re-layouts: 1.49 us -> none  [body(): wgrad = wgrad.transpose(1, 0, 2, 3).reshape(2, 2, 32, 128)]
where the time goes in v2:
time: 45 us; the launch traced here: 44.8 us
  Pallas kernels  44.2 us (98%)
  between operations  0.65 us (1%)
    pallas_call x1, Pallas kernels, body(): pl.pallas_call(functools.partial(kernel, slabs, groups), out_shape=(jax.S...  42.7 us
    pallas_call x1, Pallas kernels, body(): pl.pallas_call(expand, out_shape=(jax.ShapeDtypeStruct((256, 8, 256), BF1...  1.49 us

profile of v2, /device:TPU:1, one launch (start us, length us, event | category | flops | bytes accessed | tf_op | source)
XLA Modules:
  0.0 44.8 jit_solution(9731141303140015423)
XLA Ops:
  0.6 0.0 copy-start
  0.6 42.7 %shard_map.68 = (bf16[2,16,2,16,128]{4,3,2,1,0:T(8,128)(2,1)S(1)}, f32[2,32,2,128]{3,2,1,0:T(2,128)S(1)}) custom-call(bf16[256,8,256]{2,1,0:T(8,128)(2,1)} %bitcast.5, bf16[256,8,256]{2,1,0:T(8,128)(2,1)} %bitcast.6, bf16[64,64,128]{2,1,0:T(8,128)(2,1)} %bitcast.7, bf16[2048,256]{1,0:T(8,128)(2,1)} %constant.5.clone.tab_hbm), custom_call_target="tpu_custom_call" | custom-call | tf_op jit(solution)/shard_map/pallas_call | solution.py:319
  43.3 0.0 copy-done
  43.3 1.5 %shard_map.69 = (bf16[256,8,256]{2,1,0:T(8,128)(2,1)}, f32[2,32,2,128]{3,2,1,0:T(2,128)}) custom-call(bf16[2,16,2,16,128]{4,3,2,1,0:T(8,128)(2,1)S(1)} %get-tuple-element.6.got_ref, bf16[64,256]{1,0:T(8,128)(2,1)S(1)} %copy-done, f32[2,32,2,128]{3,2,1,0:T(2,128)S(1)} %get-tuple-element.7.wgrad_ref), custom_call_target="tpu_custom_call" | custom-call | tf_op jit(solution)/shard_map/pallas_call | solution.py:356
Async XLA Ops:
  0.6 42.7 %copy-start = (bf16[64,256]{1,0:T(8,128)(2,1)S(1)}, bf16[64,256]{1,0:T(8,128)(2,1)}, u32[]{:S(2)}) copy-start(bf16[64,256]{1,0:T(8,128)(2,1)} %constant.4.clone.ty_ref) | copy-start | bytes 98308

commit v3 on v2

--- a/solution.py
+++ b/solution.py
@@ -44,13 +44,6 @@
 RING = (4, 3, 5, 2, 6, 1, 7, 0)
 
 
-def slab_peers(me):
-    part, along = lax.div(me, 8), lax.rem(me, 8)
-    parts = [lax.rem(part + n, 2) * 8 for n in range(2)]
-    peers = [parts[n] + lax.rem(along + off, 8) for off in RING for n in (1, 0)]
-    return peers[:-1]
-
-
 def dp_peers(me):
     part, along, core = lax.div(me, 16), lax.rem(lax.div(me, 2), 8), lax.rem(me, 2)
     parts = [lax.rem(part + n, 2) * 16 for n in range(2)]
@@ -73,11 +66,11 @@
 def kernel(
     slabs, groups,
     act_hbm, cot_hbm, w_hbm, tab_hbm,
-    got_e, wgrad_ref,
+    grad_ref, wgrad_ref,
     ty_ref, fx_ref, tx_ref, act_v, cot_v, w_v, wm, lines, folded,
-    send_a, send_c, got_a, got_c, send_e,
+    send_a, send_c, got_a, got_c, send_e, got_e,
     spectra, pair_a, pair_c, all_a, all_c, stacked, mixed, sums, wsend,
-    load_sem, send_sem, recv_sem,
+    load_sem, send_sem, recv_sem, ready, ready_d,
 ):
     me_s = lax.axis_index("slab")
     me_d = lax.axis_index("dp")
@@ -98,11 +91,58 @@
     for load in loads:
         load.start()
 
-    peers_s, peers_d = slab_peers(me_s), dp_peers(me_d)
+    peers_d = dp_peers(me_d)
     barrier = pltpu.get_barrier_semaphore()
-    for axis, peers in (("slab", peers_s), ("dp", peers_d)):
-        for peer in peers:
-            pl.semaphore_signal(barrier, inc=1, device_id={axis: peer}, device_id_type=MESH)
+    part, mine = lax.div(me_s, 8), lax.rem(me_s, 8)
+    levels = slabs // 2
+    partner = lax.rem(part + 1, 2) * 8 + mine
+
+    def to_slab(sem, peer):
+        pl.semaphore_signal(sem, inc=1, device_id={"slab": peer}, device_id_type=MESH)
+
+    def to_dp(sem, peer):
+        pl.semaphore_signal(sem, inc=1, device_id={"dp": peer}, device_id_type=MESH)
+
+    for level in range(1, levels):
+        @pl.when(mine < level)
+        def _():
+            for n in range(2):
+                to_slab(barrier, n * 8 + level)
+
+    to_slab(barrier, partner)
+
+    for peer in range(1, groups):
+        @pl.when(me_d < peer)
+        def _():
+            to_dp(barrier, peer)
+
+    pl.semaphore_wait(barrier, 2 * mine + 1 + me_d)
+    for level in range(levels - 1):
+        @pl.when(level < mine)
+        def _():
+            for n in range(2):
+                to_slab(ready.at[mine], n * 8 + level)
+
+    for peer in range(groups - 1):
+        @pl.when(peer < me_d)
+        def _():
+            to_dp(ready_d, peer)
+
+
+    def send_slab(peer, src, dst, n):
+        pltpu.make_async_remote_copy(
+            src_ref=src.at[:, peer], dst_ref=dst.at[:, me_s],
+            send_sem=send_sem.at[n], recv_sem=recv_sem.at[n],
+            device_id={"slab": peer}, device_id_type=MESH,
+        ).start()
+
+    def send_earlier(src, dst, n):
+        send_slab(partner, src, dst, n)
+        for level in range(levels - 1):
+            @pl.when(level < mine)
+            def _():
+                for half in range(2):
+                    send_slab(half * 8 + level, src, dst, n)
 
     def exchange(axis, me, peers, src, dst, n, rank=0):
         lead = (slice(None),) * rank
@@ -117,7 +157,13 @@
         part = ref.at[pl.ds(0, count - 1)] if ref.shape[0] == count else ref.at[:, pl.ds(0, count - 1)]
         pltpu.make_async_copy(part, part, sem).wait()
 
-    over_slab = functools.partial(exchange, "slab", me_s, peers_s)
+
+    def over_slab(src, dst, n):
+        for off in RING[:-1]:
+            for half in range(2):
+                send_slab(half * 8 + lax.rem(mine + off, 8), src, dst, n)
+        send_slab(partner, src, dst, n)
+
     over_dp = functools.partial(exchange, "dp", me_d, peers_d)
 
     def along_y(field, send, h):
@@ -135,19 +181,25 @@
     loads[0].wait()
     loads[1].wait()
     along_y(cot_v, send_c, 0)
-    pl.semaphore_wait(barrier, slabs + groups - 2)
-    over_slab(send_c.at[0], got_c.at[0], 0)
     loads[2].wait()
     along_y(cot_v, send_c, 1)
-    over_slab(send_c.at[1], got_c.at[1], 1)
+    send_earlier(send_c, got_c, 0)
     for h in range(2):
         got_c[h, me_s] = send_c[h, me_s]
     loads[3].wait()
     along_y(act_v, send_a, 0)
     along_y(act_v, send_a, 1)
-    over_slab(send_a, got_a, 2, rank=1)
+    send_earlier(send_a, got_a, 2)
     for h in range(2):
         got_a[h, me_s] = send_a[h, me_s]
+    for level in range(1, levels):
+        @pl.when(mine < level)
+        def _():
+            pl.semaphore_wait(ready.at[level], 2)
+            for half in range(2):
+                send_slab(half * 8 + level, send_c, got_c, 0)
+            for half in range(2):
+                send_slab(half * 8 + level, send_a, got_a, 2)
 
     loads[4].wait()
     for c in range(8):
@@ -184,8 +236,7 @@
                     ]
         pair[...] = spectra[...].astype(BF16).reshape(groups, 256 // groups, 128)
 
-    wait_all(got_c.at[0], slabs, recv_sem.at[0])
-    wait_all(got_c.at[1], slabs, recv_sem.at[1])
+    wait_all(got_c, slabs, recv_sem.at[0])
     loads[5].wait()
     loads[6].wait()
     specs = spec_of(got_c)
@@ -232,16 +283,20 @@
             )
     for h in range(2):
         got_e[h, me_s] = send_e[h, me_s]
-    over_slab(send_e, got_e, 3, rank=1)
 
     to_pair(specs, pair_c)
     all_c[me_d] = pair_c[me_d]
+    @pl.when(me_d < groups - 1)
+    def _():
+        pl.semaphore_wait(ready_d, groups - 1 - me_d)
+
     over_dp(pair_c, all_c, 4)
 
     wait_all(got_a, slabs, recv_sem.at[2])
     to_pair(spec_of(got_a), pair_a)
     all_a[me_d] = pair_a[me_d]
     over_dp(pair_a, all_a, 5)
+    over_slab(send_e, got_e, 3)
 
     wait_all(all_c, groups, recv_sem.at[4])
     wait_all(all_a, groups, recv_sem.at[5])
@@ -275,38 +330,36 @@
     over_dp(wsend, wgrad_ref, 6, rank=1)
 
     wait_all(got_e, slabs, recv_sem.at[3])
+    for h in range(2):
+        folded[...] = got_e[h].astype(F32).reshape(512, 128)
+        for r in range(8):
+            values = tn(folded[pl.ds(r, 64, stride=8), :].astype(BF16), ty_ref[...])
+            for half in range(2):
+                lines[half, pl.ds(r, 128, stride=8), :] = values[
+                    :, half * 128 : half * 128 + 128
+                ]
+        for c in range(4):
+            grad_ref[h * 128 + c * 32 : h * 128 + (c + 1) * 32] = (
+                jnp.concatenate(
+                    [lines[half, c * 256 : (c + 1) * 256, :] for half in range(2)], axis=1
+                )
+                .astype(BF16)
+                .reshape(32, 8, 256)
+            )
     wait_all(wgrad_ref, groups, recv_sem.at[6])
-    for n, ref in enumerate((send_c.at[0], send_c.at[1], send_a, send_e)):
+    for n, ref in ((0, send_c), (2, send_a), (3, send_e)):
         wait_all(ref, slabs, send_sem.at[n])
     for n, ref in enumerate((pair_c, pair_a, wsend)):
         wait_all(ref, groups, send_sem.at[4 + n])
 
 
-def expand(got_ref, ty_ref, wgrad_ref, grad_hbm, wgrad_hbm, folded, lines, grad_v, sems):
-    copies = [pltpu.make_async_copy(wgrad_ref, wgrad_hbm, sems.at[0])]
-    copies[0].start()
-    for h in range(2):
-        folded[h] = got_ref[h].astype(F32).reshape(512, 128)
-        for r in range(8):
-            values = tn(folded[h, pl.ds(r, 64, stride=8), :].astype(BF16), ty_ref[...])
-            for half in range(2):
-                lines[h, half, pl.ds(r, 128, stride=8), :] = values[
-                    :, half * 128 : half * 128 + 128
-                ]
-        for c in range(4):
-            grad_v[h, c * 32 : (c + 1) * 32] = (
-                jnp.concatenate(
-                    [lines[h, half, c * 256 : (c + 1) * 256, :] for half in range(2)], axis=1
-                )
-                .astype(BF16)
-                .reshape(32, 8, 256)
-            )
-        copies.append(
-            pltpu.make_async_copy(
-                grad_v.at[h], grad_hbm.at[pl.ds(h * 128, 128)], sems.at[h + 1]
-            )
-        )
-        copies[-1].start()
+def passed(grad_ref, wgrad_ref, grad_hbm, wgrad_hbm, sems):
+    copies = [
+        pltpu.make_async_copy(grad_ref, grad_hbm, sems.at[0]),
+        pltpu.make_async_copy(wgrad_ref, wgrad_hbm, sems.at[1]),
+    ]
+    for copy in copies:
+        copy.start()
     for copy in copies:
         copy.wait()
 
@@ -318,7 +371,10 @@
     total = (2, groups, 2, 128)
     got, wgrad = pl.pallas_call(
         functools.partial(kernel, slabs, groups),
-        out_shape=(jax.ShapeDtypeStruct(block, BF16), jax.ShapeDtypeStruct(total, F32)),
+        out_shape=(
+            jax.ShapeDtypeStruct((256, 8, 256), BF16),
+            jax.ShapeDtypeStruct(total, F32),
+        ),
         in_specs=[pl.BlockSpec(memory_space=pltpu.HBM)] * 4,
         out_specs=[pl.BlockSpec(memory_space=pltpu.VMEM)] * 2,
         scratch_shapes=[
@@ -332,7 +388,7 @@
             pltpu.VMEM((2, 2048, 128), F32),
             pltpu.VMEM((512, 128), F32),
         ]
-        + [pltpu.VMEM(block, BF16)] * 5
+        + [pltpu.VMEM(block, BF16)] * 6
         + [pltpu.VMEM((256, 128), F32)]
         + [pltpu.VMEM(pair, BF16)] * 4
         + [
@@ -343,9 +399,11 @@
             pltpu.SemaphoreType.DMA((7,)),
             pltpu.SemaphoreType.DMA((7,)),
             pltpu.SemaphoreType.DMA((7,)),
+            pltpu.SemaphoreType.REGULAR((slabs // 2,)),
+            pltpu.SemaphoreType.REGULAR,
         ],
         compiler_params=pltpu.CompilerParams(
-            collective_id=0, has_side_effects=True, vmem_limit_bytes=67043328 - 11300000
+            collective_id=0, has_side_effects=True, vmem_limit_bytes=67043328 - 12200000
         ),
     )(
         activation.reshape(256, 8, 256),
@@ -354,18 +412,13 @@
         packed,
     )
     grad, wgrad = pl.pallas_call(
-        expand,
+        passed,
         out_shape=(jax.ShapeDtypeStruct((256, 8, 256), BF16), jax.ShapeDtypeStruct(total, F32)),
-        in_specs=[pl.BlockSpec(memory_space=pltpu.VMEM)] * 3,
+        in_specs=[pl.BlockSpec(memory_space=pltpu.VMEM)] * 2,
         out_specs=[pl.BlockSpec(memory_space=pltpu.HBM)] * 2,
-        scratch_shapes=[
-            pltpu.VMEM((2, 512, 128), F32),
-            pltpu.VMEM((2, 2, 1024, 128), F32),
-            pltpu.VMEM((2, 128, 8, 256), BF16),
-            pltpu.SemaphoreType.DMA((3,)),
-        ],
+        scratch_shapes=[pltpu.SemaphoreType.DMA((2,))],
         compiler_params=pltpu.CompilerParams(vmem_limit_bytes=20 << 20),
-    )(got, ty, wgrad)
+    )(got, wgrad)
     return grad.reshape(4, 64, 8, 256), wgrad.reshape(2, 2, 32, 128)
 
 

time: 45 us -> 43.1 us (0.958)
  the two profiles are of different devices: /device:TPU:1 before, /device:TPU:2 now
where the time goes in v3:
time: 43.1 us; the launch traced here: 42.9 us
  Pallas kernels  42.3 us (98%)
  between operations  0.64 us (1%)
    pallas_call x1, Pallas kernels, body(): pl.pallas_call(functools.partial(kernel, slabs, groups), out_shape=(jax.S...  41.3 us
    pallas_call x1, Pallas kernels, body(): pl.pallas_call(passed, out_shape=(jax.ShapeDtypeStruct((256, 8, 256), BF1...  0.99 us

profile of v3, /device:TPU:2, one launch (start us, length us, event | category | flops | bytes accessed | tf_op | source)
XLA Modules:
  0.0 42.9 jit_solution(12285984031423658143)
XLA Ops:
  0.6 41.3 %shard_map.59 = (bf16[256,8,256]{2,1,0:T(8,128)(2,1)S(1)}, f32[2,32,2,128]{3,2,1,0:T(2,128)S(1)}) custom-call(bf16[256,8,256]{2,1,0:T(8,128)(2,1)} %bitcast.5, bf16[256,8,256]{2,1,0:T(8,128)(2,1)} %bitcast.6, bf16[64,64,128]{2,1,0:T(8,128)(2,1)} %bitcast.7, bf16[2048,256]{1,0:T(8,128)(2,1)} %constant.2.clone.tab_hbm), custom_call_target="tpu_custom_call" | custom-call | tf_op jit(solution)/shard_map/pallas_call | solution.py:372
  42.0 1.0 %shard_map.60 = (bf16[256,8,256]{2,1,0:T(8,128)(2,1)}, f32[2,32,2,128]{3,2,1,0:T(2,128)}) custom-call(bf16[256,8,256]{2,1,0:T(8,128)(2,1)S(1)} %get-tuple-element.6.grad_ref, f32[2,32,2,128]{3,2,1,0:T(2,128)S(1)} %get-tuple-element.7.wgrad_ref), custom_call_target="tpu_custom_call" | custom-call | tf_op jit(solution)/shard_map/pallas_call | solution.py:414

commit v4 on v3

--- a/solution.py
+++ b/solution.py
@@ -70,7 +70,7 @@
     ty_ref, fx_ref, tx_ref, act_v, cot_v, w_v, wm, lines, folded,
     send_a, send_c, got_a, got_c, send_e, got_e,
     spectra, pair_a, pair_c, all_a, all_c, stacked, mixed, sums, wsend,
-    load_sem, send_sem, recv_sem, ready, ready_d,
+    load_sem, send_sem, recv_sem, ready, near, four, passed_on,
 ):
     me_s = lax.axis_index("slab")
     me_d = lax.axis_index("dp")
@@ -92,6 +92,7 @@
         load.start()
 
     peers_d = dp_peers(me_d)
+    rows_y = groups // 4
     barrier = pltpu.get_barrier_semaphore()
     part, mine = lax.div(me_s, 8), lax.rem(me_s, 8)
     levels = slabs // 2
@@ -111,23 +112,52 @@
 
     to_slab(barrier, partner)
 
-    for peer in range(1, groups):
-        @pl.when(me_d < peer)
-        def _():
-            to_dp(barrier, peer)
-
-    pl.semaphore_wait(barrier, 2 * mine + 1 + me_d)
+    core, row, side = lax.rem(me_d, 2), lax.rem(lax.div(me_d, 2), rows_y), lax.div(me_d, 2 * rows_y)
+    last = rows_y - 1
+    for earlier, step in ((core == 0, 1), (side == 0, 2 * rows_y), (row < last, 2)):
+        @pl.when(earlier)
+        def _():
+            to_dp(barrier, me_d + step)
+
+    pl.semaphore_wait(barrier, 2 * mine + 1 + core + side + lax.div(row + last, rows_y))
     for level in range(levels - 1):
         @pl.when(level < mine)
         def _():
             for n in range(2):
                 to_slab(ready.at[mine], n * 8 + level)
 
-    for peer in range(groups - 1):
-        @pl.when(peer < me_d)
-        def _():
-            to_dp(ready_d, peer)
-
+    for later, step in ((core == 1, 1), (side == 1, 2 * rows_y), (row > 0, 2)):
+        @pl.when(later)
+        def _():
+            to_dp(near, me_d - step)
+
+
+    def meet_four():
+        count = 2 - core - side + lax.div(2 * last - row - 1, last)
+
+        @pl.when(count > 0)
+        def _():
+            pl.semaphore_wait(near, count)
+
+        to_dp(four, side * 2 * rows_y + row * 2 + 1 - core)
+        to_dp(four, (1 - side) * 2 * rows_y + row * 2 + core)
+
+    def scan(upward):
+        first, final = (row > 0, row < last) if upward else (row < last, row > 0)
+
+        @pl.when(first)
+        def _():
+            pl.semaphore_wait(passed_on.at[int(upward)], 1)
+
+        @pl.when(final)
+        def _():
+            to_dp(passed_on.at[int(upward)], me_d + 2 if upward else me_d - 2)
+
+    def meet_half(which):
+        for low_half in (True, False):
+            @pl.when((row < rows_y // 2) if low_half else (row >= rows_y // 2))
+            def _():
+                scan(low_half == (which == 0))
 
     def send_slab(peer, src, dst, n):
         pltpu.make_async_remote_copy(
@@ -192,6 +222,7 @@
     send_earlier(send_a, got_a, 2)
     for h in range(2):
         got_a[h, me_s] = send_a[h, me_s]
+    meet_four()
     for level in range(1, levels):
         @pl.when(mine < level)
         def _():
@@ -201,6 +232,8 @@
             for half in range(2):
                 send_slab(half * 8 + level, send_a, got_a, 2)
 
+    pl.semaphore_wait(four, 2)
+    meet_half(0)
     loads[4].wait()
     for c in range(8):
         part = w_v[c * 8 : (c + 1) * 8].astype(F32).reshape(512, 128)
@@ -236,6 +269,7 @@
                     ]
         pair[...] = spectra[...].astype(BF16).reshape(groups, 256 // groups, 128)
 
+    meet_half(1)
     wait_all(got_c, slabs, recv_sem.at[0])
     loads[5].wait()
     loads[6].wait()
@@ -286,10 +320,6 @@
 
     to_pair(specs, pair_c)
     all_c[me_d] = pair_c[me_d]
-    @pl.when(me_d < groups - 1)
-    def _():
-        pl.semaphore_wait(ready_d, groups - 1 - me_d)
-
     over_dp(pair_c, all_c, 4)
 
     wait_all(got_a, slabs, recv_sem.at[2])
@@ -353,7 +383,7 @@
         wait_all(ref, groups, send_sem.at[4 + n])
 
 
-def passed(grad_ref, wgrad_ref, grad_hbm, wgrad_hbm, sems):
+def write_out(grad_ref, wgrad_ref, grad_hbm, wgrad_hbm, sems):
     copies = [
         pltpu.make_async_copy(grad_ref, grad_hbm, sems.at[0]),
         pltpu.make_async_copy(wgrad_ref, wgrad_hbm, sems.at[1]),
@@ -401,6 +431,8 @@
             pltpu.SemaphoreType.DMA((7,)),
             pltpu.SemaphoreType.REGULAR((slabs // 2,)),
             pltpu.SemaphoreType.REGULAR,
+            pltpu.SemaphoreType.REGULAR,
+            pltpu.SemaphoreType.REGULAR((2,)),
         ],
         compiler_params=pltpu.CompilerParams(
             collective_id=0, has_side_effects=True, vmem_limit_bytes=67043328 - 12200000
@@ -412,7 +444,7 @@
         packed,
     )
     grad, wgrad = pl.pallas_call(
-        passed,
+        write_out,
         out_shape=(jax.ShapeDtypeStruct((256, 8, 256), BF16), jax.ShapeDtypeStruct(total, F32)),
         in_specs=[pl.BlockSpec(memory_space=pltpu.VMEM)] * 2,
         out_specs=[pl.BlockSpec(memory_space=pltpu.HBM)] * 2,

time: 43.1 us -> 39 us (0.905)
  the two profiles are of different devices: /device:TPU:2 before, /device:TPU:1 now
where the time goes in v4:
time: 39 us; the launch traced here: 38.7 us
  Pallas kernels  38 us (97%)
  between operations  0.64 us (2%)
    pallas_call x1, Pallas kernels, body(): pl.pallas_call(functools.partial(kernel, slabs, groups), out_shape=(jax.S...  37 us
    pallas_call x1, Pallas kernels, body(): pl.pallas_call(write_out, out_shape=(jax.ShapeDtypeStruct((256, 8, 256),...  0.99 us

profile of v4, /device:TPU:1, one launch (start us, length us, event | category | flops | bytes accessed | tf_op | source)
XLA Modules:
  0.0 38.7 jit_solution(4113449755229264597)
XLA Ops:
  0.6 37.0 %shard_map.59 = (bf16[256,8,256]{2,1,0:T(8,128)(2,1)S(1)}, f32[2,32,2,128]{3,2,1,0:T(2,128)S(1)}) custom-call(bf16[256,8,256]{2,1,0:T(8,128)(2,1)} %bitcast.5, bf16[256,8,256]{2,1,0:T(8,128)(2,1)} %bitcast.6, bf16[64,64,128]{2,1,0:T(8,128)(2,1)} %bitcast.7, bf16[2048,256]{1,0:T(8,128)(2,1)} %constant.2.clone.tab_hbm), custom_call_target="tpu_custom_call" | custom-call | tf_op jit(solution)/shard_map/pallas_call | solution.py:402
  37.7 1.0 %shard_map.60 = (bf16[256,8,256]{2,1,0:T(8,128)(2,1)}, f32[2,32,2,128]{3,2,1,0:T(2,128)}) custom-call(bf16[256,8,256]{2,1,0:T(8,128)(2,1)S(1)} %get-tuple-element.6.grad_ref, f32[2,32,2,128]{3,2,1,0:T(2,128)S(1)} %get-tuple-element.7.wgrad_ref), custom_call_target="tpu_custom_call" | custom-call | tf_op jit(solution)/shard_map/pallas_call | solution.py:446

commit v5 on v4

--- a/solution.py
+++ b/solution.py
@@ -323,10 +323,10 @@
     over_dp(pair_c, all_c, 4)
 
     wait_all(got_a, slabs, recv_sem.at[2])
+    over_slab(send_e, got_e, 3)
     to_pair(spec_of(got_a), pair_a)
     all_a[me_d] = pair_a[me_d]
     over_dp(pair_a, all_a, 5)
-    over_slab(send_e, got_e, 3)
 
     wait_all(all_c, groups, recv_sem.at[4])
     wait_all(all_a, groups, recv_sem.at[5])

time: 39 us -> 38.8 us (level)
  no operation moved by 1% of the time
where the time goes in v5:
time: 38.8 us; the launch traced here: 38.7 us
  Pallas kernels  38 us (98%)
  between operations  0.64 us (2%)
    pallas_call x1, Pallas kernels, body(): pl.pallas_call(functools.partial(kernel, slabs, groups), out_shape=(jax.S...  37 us
    pallas_call x1, Pallas kernels, body(): pl.pallas_call(write_out, out_shape=(jax.ShapeDtypeStruct((256, 8, 256),...  0.99 us

profile of v5, /device:TPU:1, one launch (start us, length us, event | category | flops | bytes accessed | tf_op | source)
XLA Modules:
  0.0 38.7 jit_solution(16230363437042344721)
XLA Ops:
  0.6 37.0 %shard_map.59 = (bf16[256,8,256]{2,1,0:T(8,128)(2,1)S(1)}, f32[2,32,2,128]{3,2,1,0:T(2,128)S(1)}) custom-call(bf16[256,8,256]{2,1,0:T(8,128)(2,1)} %bitcast.5, bf16[256,8,256]{2,1,0:T(8,128)(2,1)} %bitcast.6, bf16[64,64,128]{2,1,0:T(8,128)(2,1)} %bitcast.7, bf16[2048,256]{1,0:T(8,128)(2,1)} %constant.2.clone.tab_hbm), custom_call_target="tpu_custom_call" | custom-call | tf_op jit(solution)/shard_map/pallas_call | solution.py:402
  37.7 1.0 %shard_map.60 = (bf16[256,8,256]{2,1,0:T(8,128)(2,1)}, f32[2,32,2,128]{3,2,1,0:T(2,128)}) custom-call(bf16[256,8,256]{2,1,0:T(8,128)(2,1)S(1)} %get-tuple-element.6.grad_ref, f32[2,32,2,128]{3,2,1,0:T(2,128)S(1)} %get-tuple-element.7.wgrad_ref), custom_call_target="tpu_custom_call" | custom-call | tf_op jit(solution)/shard_map/pallas_call | solution.py:446
